TPU v7x, 32 devices: a whole 2x2x4 slice. The times are simulated.
32 devices in a mesh: rep: 8 (over z, y), shard: 4 (over x, core).
Axes of the slice: x: 2, y: 2, z: 4, core: 2. Of those that a mesh axis runs over, the one named last changes fastest.
Arguments:
- activ: bfloat16 [4096, 8192], P(('rep', 'shard')), may hold values from -6 to 6
- key_grad: bfloat16 [4096, 640], P(('rep', 'shard')), may hold values from -1.1953125 to 1.1953125
- key_weight: bfloat16 [8192, 640], P('shard'), may hold values from -0.25 to 0.25
- feedback: bfloat16 [8, 40960, 128], P('rep', 'shard'), may hold values from -24 to 24
- kept: int32 [8, 4, 512], P('rep', 'shard'), may hold values from 0 to 10239, as said below
- region_len: int32 [4, 8], P('shard'), may hold values from 640 to 1920, as said below
Outputs:
- input_grad: bfloat16 [4096, 8192], P(('rep', 'shard'))
- next_feedback: bfloat16 [8, 40960, 128], P('rep', 'shard')
- owned_sum: float32 [4, 15360, 128], P('shard', 'rep')
Inputs may be any that keep to these rules, and one draw needn't show every extreme that they name: `region_len`: each row splits its shard's 10240 blocks into 8 regions in order of owner and sums to 10240; every row has a region of exactly 1920 blocks. `kept`: the 512 numbers of a row are different blocks of that shard. At most 128 of them lie in one region of the shard; every row has exactly 128 in some region, and in every shard some region gets exactly 128 from every replica.
All inputs are finite; a program needn't handle non-finite values.
Results may differ from a plain program's by a relative error of at most 0.011.
Values may be sent and summed in bfloat16 or wider, within the bound.
A program may use at most 128 MiB of HBM per device.

v0:
```python
import jax
import jax.numpy as jnp
from jax import lax
from jax.sharding import PartitionSpec as P


def accumulate(block_rows, block_ids, own_start, own_len, region_max):
    offset = block_ids - own_start
    inside = (offset >= 0) & (offset < own_len)
    target = jnp.where(inside, offset, region_max)
    blank = jnp.zeros((region_max, block_rows.shape[1]), jnp.float32)
    return blank.at[target].add(block_rows.astype(jnp.float32), mode="drop")


def per_device(activ, key_grad, key_weight, feedback, kept, region_len):
    grads_all = lax.all_gather(key_grad, "shard", axis=0, tiled=True)
    act_cols = lax.all_to_all(activ, "shard", split_axis=1, concat_axis=0, tiled=True)
    weight_grad = lax.dot_general(
        act_cols, grads_all, (((0,), (0,)), ((), ())), preferred_element_type=jnp.float32
    )
    input_cols = lax.dot_general(
        grads_all, key_weight, (((1,), (1,)), ((), ())), preferred_element_type=jnp.float32
    ).astype(jnp.bfloat16)
    input_grad = lax.all_to_all(input_cols, "shard", split_axis=0, concat_axis=1, tiled=True)
    table = feedback[0]
    chosen = kept[0, 0]
    lengths = region_len[0]
    replicas = lax.axis_size("rep")
    block_count = table.shape[0]
    block_size = table.shape[1]
    keep_count = chosen.shape[0]
    mean_len = block_count // replicas
    region_max = mean_len + mean_len // 2
    starts = jnp.cumsum(lengths) - lengths
    owner_self = lax.axis_index("rep")
    own_start = starts[owner_self]
    own_len = lengths[owner_self]
    kept_rows = table[chosen]
    flags = jnp.zeros((block_count,), bool).at[chosen].set(True)
    cleared = jnp.where(flags[:, None], jnp.float32(0.0), table.astype(jnp.float32))
    next_feedback = (cleared + weight_grad.reshape(block_count, block_size)).astype(jnp.bfloat16)[
        None
    ]
    owner_id = jnp.sum((starts[None, :] <= chosen[:, None]).astype(jnp.int32), axis=1) - 1
    serial = jnp.arange(keep_count, dtype=jnp.int32)
    earlier = (owner_id[:, None] == owner_id[None, :]) & (serial[None, :] < serial[:, None])
    slot_index = jnp.sum(earlier.astype(jnp.int32), axis=1)
    capacity = 2 * keep_count // replicas
    place_at = owner_id * capacity + slot_index
    send_rows = (
        jnp.zeros((replicas * capacity, block_size), jnp.bfloat16).at[place_at].set(kept_rows)
    )
    send_ids = jnp.full((replicas * capacity,), -1, jnp.int32).at[place_at].set(chosen)
    got_rows, got_ids = (
        lax.all_to_all(send_rows, "rep", split_axis=0, concat_axis=0, tiled=True),
        lax.all_to_all(send_ids, "rep", split_axis=0, concat_axis=0, tiled=True),
    )
    owned_rows = accumulate(got_rows, got_ids, own_start, own_len, region_max)
    return (input_grad, next_feedback, owned_rows[None])


def solution(mesh):
    return jax.shard_map(
        per_device,
        mesh=mesh,
        in_specs=(
            P(("rep", "shard"), None),
            P(("rep", "shard"), None),
            P("shard", None),
            P("rep", "shard", None),
            P("rep", "shard", None),
            P("shard", None),
        ),
        out_specs=(P(("rep", "shard"), None), P("rep", "shard", None), P("shard", "rep", None)),
        check_vma=False,
    )
```

profile of v0, /device:TPU:0, one launch (start us, length us, event | category | flops | bytes accessed | tf_op | source)
XLA Modules:
  0.0 117.7 jit_solution(1622688939139694994)
XLA Ops:
  0.6 1.0 reduce-window.4
  1.6 0.7 fusion.11
  2.3 0.8 convert_reduce_fusion.1
  3.3 3.2 %scatter_custom_fusion.1 = s32[1024]{0:T(1024)} fusion(s32[512]{0:T(512)S(1)} %bitcast.56, s32[512]{0:T(512)} %bitcast.54, s32[]{:T(128)} %constant.18.clone.1), kind=kCustom, calls=%fused_computation.26 | custom fusion | bytes 4608 | tf_op jit(solution)/shard_map/scatter | solution.py:53
  6.5 7.3 %all-to-all-start.2 = ((s32[8,128,1]{1,2,0:T(1,128)}), s32[8,128,1]{1,2,0:T(1,128)S(1)}, u32[]{:S(2)}, u32[]{:S(2)}) async-start(s32[8,128,1]{1,2,0:T(1,128)} %bitcast.14), calls=%async_computation.2 | async-start | bytes 8192 | tf_op jit(solution)/shard_map/all_to_all | solution.py:56
  13.8 0.7 compare_select_fusion.2
  15.1 5.5 %scatter_custom_fusion.2 = bf16[1024,128]{1,0:T(8,128)(2,1)} fusion(s32[512]{0:T(512)S(1)} %bitcast.57, bf16[]{:T(256)} %constant.12.clone.1, bf16[10240,128]{1,0:T(8,128)(2,1)} %bitcast.43, s32[1024]{0:T(1024)S(1)} %pad_clamp_fusion), kind=kCustom, calls=%fused_computation.13 | custom fusion | bytes 262656 | tf_op jit(solution)/shard_map/scatter | solution.py:51
  20.6 6.0 %all-to-all-start.3 = ((bf16[8,128,128]{2,1,0:T(8,128)(2,1)}), bf16[8,128,128]{2,1,0:T(8,128)(2,1)S(1)}, u32[]{:S(2)}, u32[]{:S(2)}) async-start(bf16[8,128,128]{2,1,0:T(8,128)(2,1)} %bitcast.23), calls=%async_computation.3 | async-start | bytes 524288 | tf_op jit(solution)/shard_map/all_to_all | solution.py:55
  26.6 4.1 %copy.20 = bf16[128,8192]{0,1:T(8,128)(2,1)} copy(bf16[128,8192]{1,0:T(8,128)(2,1)} %param.6) | data formatting | bytes 4194304 | tf_op args[0]
  30.7 4.4 %all-to-all-done.3 = bf16[8,128,128]{2,1,0:T(8,128)(2,1)S(1)} async-done(((bf16[8,128,128]{2,1,0:T(8,128)(2,1)}), bf16[8,128,128]{2,1,0:T(8,128)(2,1)S(1)}, u32[]{:S(2)}, u32[]{:S(2)}) %all-to-all-start.3) | async-done | bytes 262176 | tf_op jit(solution)/shard_map/all_to_all | solution.py:55
  35.1 4.4 %all-to-all-start.1 = ((bf16[128,4,2048]{0,2,1:T(8,128)(2,1)}), bf16[128,4,2048]{0,2,1:T(8,128)(2,1)}, u32[]{:S(2)}, u32[]{:S(2)}) async-start(bf16[128,4,2048]{0,2,1:T(8,128)(2,1)} %bitcast.42), calls=%async_computation.1 | async-start | bytes 4194304 | tf_op jit(solution)/shard_map/all_to_all | solution.py:17
  39.6 30.0 %all_gather.3 = bf16[512,640]{1,0:T(8,128)(2,1)S(1)} all-gather(bf16[128,640]{1,0:T(8,128)(2,1)} %param.7), channel_id=1, replica_groups=mesh['rep'=8,'shard'=4] {'shard'}, dimensions={0}, use_global_device_ids=true | all-gather | bytes 819200 | tf_op jit(solution)/shard_map/all_gather | solution.py:16
  69.6 3.1 %convolution_convert_fusion = bf16[512,2048]{1,0:T(8,128)(2,1)} fusion(bf16[512,640]{1,0:T(8,128)(2,1)S(1)} %all_gather.3, bf16[2048,640]{1,0:T(8,128)(2,1)S(1)} %copy-done), kind=kOutput, calls=%fused_computation.6 | convolution fusion | flops 1343225856 | bytes 5373952 | tf_op jit(solution)/shard_map/dot_general | solution.py:21
  72.7 4.6 %all-to-all-start = ((bf16[4,128,2048]{2,1,0:T(8,128)(2,1)}), bf16[4,128,2048]{2,1,0:T(8,128)(2,1)}, u32[]{:S(2)}, u32[]{:S(2)}) async-start(bf16[4,128,2048]{2,1,0:T(8,128)(2,1)} %bitcast.44), calls=%async_computation | async-start | bytes 4194304 | tf_op jit(solution)/shard_map/all_to_all | solution.py:24
  77.4 0.6 constant_dynamic-slice_fusion
  79.1 2.6 %scatter_custom_fusion = pred[10240]{0:T(1024)(128)(4,1)S(1)} fusion(s32[512]{0:T(512)} %bitcast.51, pred[512]{0:T(512)(128)(4,1)} %broadcast.121, pred[]{:T(512)} %constant.13.clone.1), kind=kCustom, calls=%fused_computation.17 | custom fusion | bytes 10752 | tf_op jit(solution)/shard_map/scatter | solution.py:39
  81.7 0.7 broadcast_subtract_fusion
  82.3 0.6 compare_select_fusion
  83.0 7.0 %scatter_custom_fusion.3 = f32[1920,128]{1,0:T(8,128)} fusion(s32[1024]{0:T(1024)S(1)} %bitcast.55, bf16[1024,128]{1,0:T(8,128)(2,1)S(1)} %bitcast.46, f32[]{:T(128)} %constant.17.clone.1), kind=kCustom, calls=%fused_computation.10 | custom fusion | flops 262144 | bytes 1245188 | tf_op jit(solution)/shard_map/scatter-add | solution.py:12
  90.0 3.9 %copy.21 = bf16[4,128,2048]{2,1,0:T(8,128)(2,1)} copy(bf16[4,128,2048]{1,2,0:T(8,128)(2,1)} %bitcast.5) | data formatting | bytes 4194304 | tf_op jit(solution)/shard_map/all_to_all | solution.py:17
  93.9 5.8 %fusion.12 = f32[2048,640]{1,0:T(8,128)} fusion(bf16[512,2048]{1,0:T(8,128)(2,1)} %bitcast.41, bf16[512,640]{1,0:T(8,128)(2,1)S(1)} %all_gather.3), kind=kOutput, calls=%fused_computation.33 | convolution fusion | flops 1342177280 | bytes 7995392 | tf_op jit(solution)/shard_map/dot_general | solution.py:18
  99.7 6.5 %reshape.138 = f32[1,10240,128]{2,1,0:T(8,128)} reshape(f32[2048,640]{1,0:T(8,128)} %fusion.12) | data formatting | bytes 10485760 | tf_op jit(solution)/shard_map/reshape | solution.py:41
  106.2 3.3 %copy.24 = bf16[4,16,8,2048]{3,2,0,1:T(8,128)(2,1)} copy(bf16[4,16,8,2048]{3,2,1,0:T(8,128)(2,1)} %bitcast.28) | data formatting | bytes 4194304 | tf_op jit(solution)/shard_map/all_to_all | solution.py:24
  109.5 8.2 %add_convert_fusion = bf16[1,10240,128]{2,1,0:T(8,128)(2,1)} fusion(f32[1,10240,128]{2,1,0:T(8,128)} %reshape.138, bf16[1,10240,128]{2,1,0:T(8,128)(2,1)S(1)} %copy-done.1, pred[10240]{0:T(1024)(128)(4,1)S(1)} %scatter_custom_fusion), kind=kLoop, calls=%fused_computation.5 | loop fusion | flops 5242880 | bytes 10496000 | tf_op jit(solution)/shard_map/convert_element_type | solution.py:41
  (19 shorter events, 2.0 us)
Async XLA Ops:
  0.6 68.9 %copy-start = (bf16[2048,640]{1,0:T(8,128)(2,1)S(1)}, bf16[2048,640]{1,0:T(8,128)(2,1)}, u32[]{:S(2)}) copy-start(bf16[2048,640]{1,0:T(8,128)(2,1)} %param.8) | copy-start | bytes 7864324
  6.5 14.1 %all-to-all-start.2 = ((s32[8,128,1]{1,2,0:T(1,128)}), s32[8,128,1]{1,2,0:T(1,128)S(1)}, u32[]{:S(2)}, u32[]{:S(2)}) async-start(s32[8,128,1]{1,2,0:T(1,128)} %bitcast.14), calls=%async_computation.2 | async-start | bytes 8192 | tf_op jit(solution)/shard_map/all_to_all | solution.py:56
  14.5 0.6 copy-start.2
  20.6 14.5 %all-to-all-start.3 = ((bf16[8,128,128]{2,1,0:T(8,128)(2,1)}), bf16[8,128,128]{2,1,0:T(8,128)(2,1)S(1)}, u32[]{:S(2)}, u32[]{:S(2)}) async-start(bf16[8,128,128]{2,1,0:T(8,128)(2,1)} %bitcast.23), calls=%async_computation.3 | async-start | bytes 524288 | tf_op jit(solution)/shard_map/all_to_all | solution.py:55
  35.1 37.6 %all-to-all-start.1 = ((bf16[128,4,2048]{0,2,1:T(8,128)(2,1)}), bf16[128,4,2048]{0,2,1:T(8,128)(2,1)}, u32[]{:S(2)}, u32[]{:S(2)}) async-start(bf16[128,4,2048]{0,2,1:T(8,128)(2,1)} %bitcast.42), calls=%async_computation.1 | async-start | bytes 4194304 | tf_op jit(solution)/shard_map/all_to_all | solution.py:17
  72.7 4.6 %copy-start.3 = (s32[1,8]{1,0:T(1,128)S(1)}, s32[1,8]{1,0:T(1,128)}, u32[]{:S(2)}) copy-start(s32[1,8]{1,0:T(1,128)} %param.11) | copy-start | bytes 100
  72.7 33.5 %all-to-all-start = ((bf16[4,128,2048]{2,1,0:T(8,128)(2,1)}), bf16[4,128,2048]{2,1,0:T(8,128)(2,1)}, u32[]{:S(2)}, u32[]{:S(2)}) async-start(bf16[4,128,2048]{2,1,0:T(8,128)(2,1)} %bitcast.44), calls=%async_computation | async-start | bytes 4194304 | tf_op jit(solution)/shard_map/all_to_all | solution.py:24
  106.2 3.3 %copy-start.1 = (bf16[1,10240,128]{2,1,0:T(8,128)(2,1)S(1)}, bf16[1,10240,128]{2,1,0:T(8,128)(2,1)}, u32[]{:S(2)}) copy-start(bf16[1,10240,128]{2,1,0:T(8,128)(2,1)} %param.9) | copy-start | bytes 7864324
where the time goes:
time: 119 us; the launch traced here: 118 us
  local copies, waits for them, and re-layouts  31.4 us (26%)
  blocking collectives  30 us (25%)
  starting transfers between devices  22.4 us (19%)
  other arithmetic  19.8 us (17%)
  matrix products  8.92 us (7%)
  waiting for transfers between devices  4.45 us (4%)
    all_gather x1, blocking collectives, per_device(): grads_all = lax.all_gather(key_grad, 'shard', axis=0, tiled=True)  30 us
    convert_element_type x1, other arithmetic, per_device(): (cleared + weight_grad.reshape(block_count, block_size)).astype(jnp.bfloa...  8.16 us
    all_to_all x1, starting transfers between devices, per_device(): lax.all_to_all(send_ids, 'rep', split_axis=0, concat_axis=0, tiled=True)  7.31 us
    scatter-add x1, other arithmetic, accumulate(): return blank.at[target].add(block_rows.astype(jnp.float32), mode='drop')  7.02 us
    reshape x1, local copies, waits for them, and re-layouts, per_device(): weight_grad.reshape(block_count, block_size)  6.47 us
    all_to_all x1, starting transfers between devices, per_device(): lax.all_to_all(send_rows, 'rep', split_axis=0, concat_axis=0, tiled=True)  6 us
    dot_general x1, matrix products, per_device(): lax.dot_general(act_cols, grads_all, (((0,), (0,)), ((), ())), preferred_...  5.78 us
    scatter x1, local copies, waits for them, and re-layouts, per_device(): jnp.zeros((replicas * capacity, block_size), jnp.bfloat16).at[place_at]  5.51 us
  transfers between devices with their start and end apart: 4, of which 1 were waited for; matrix products, arithmetic and copies ran while one was open for 36% of the time, Pallas kernels for 0%

commit v1 on v0

v1 whole, which is shorter than its diff:
```python
import functools

import jax
import jax.numpy as jnp
from jax import lax
from jax.experimental import pallas as pl
from jax.experimental.pallas import tpu as pltpu
from jax.sharding import PartitionSpec as P

MESH = pl.DeviceIdType.MESH


def flip(index, bit):
    out = index
    power = 1
    while power <= bit:
        if bit & power:
            out = out + power - 2 * power * ((index // power) % 2)
        power *= 2
    return out


def largest_divisor(total, most, step):
    best = step
    for size in range(step, most + 1, step):
        if total % size == 0:
            best = size
    return best


def kernel(
    n,
    reps,
    activ,
    key_grad,
    key_weight,
    feedback,
    chosen,
    lengths,
    input_grad,
    next_feedback,
    owned,
    grads,
    acts,
    weight,
    table,
    got_rows,
    got_ids,
    cols_out,
    columns_of,
    picked,
    grad_blocks,
    owned_buf,
    local_sem,
    grad_send,
    grad_recv,
    act_send,
    act_recv,
    out_send,
    out_recv,
    row_send,
    row_recv,
    id_send,
    id_recv,
):
    me = lax.axis_index("shard")
    rep = lax.axis_index("rep")
    tokens, feats = key_grad.shape
    width = activ.shape[1] // n
    count, size = table.shape
    keep = chosen.shape[-1]
    masks = list(range(n - 1, 0, -1))

    loads = [
        pltpu.make_async_copy(feedback.at[0], table, local_sem.at[0]),
        pltpu.make_async_copy(key_weight, weight, local_sem.at[1]),
        pltpu.make_async_copy(key_grad, grads.at[me], local_sem.at[2]),
        pltpu.make_async_copy(
            activ.at[:, pl.ds(pl.multiple_of(me * width, width), width)],
            acts.at[me],
            local_sem.at[3],
        ),
    ]
    for load in loads:
        load.start()

    barrier = pltpu.get_barrier_semaphore()
    for mask in masks:
        pl.semaphore_signal(
            barrier, inc=1, device_id={"shard": flip(me, mask)}, device_id_type=MESH
        )
    for d in range(1, reps):
        pl.semaphore_signal(
            barrier, inc=1, device_id={"rep": lax.rem(rep + d, reps)}, device_id_type=MESH
        )
    pl.semaphore_wait(barrier, n - 1 + reps - 1)

    def grad_copy(have, bit):
        block = flip(me, have)
        return pltpu.make_async_remote_copy(
            src_ref=grads.at[block] if have else key_grad,
            dst_ref=grads.at[block],
            send_sem=grad_send.at[have + bit],
            recv_sem=grad_recv.at[have + bit],
            device_id={"shard": flip(me, bit)},
            device_id_type=MESH,
        )

    bits = []
    bit = n // 2
    while bit:
        bits.append(bit)
        bit //= 2
    first = grad_copy(0, bits[0])
    first.start()
    act_copies = []
    for mask in sorted(masks, key=lambda m: m == bits[0] + 1):
        peer = flip(me, mask)
        act_copies.append(
            pltpu.make_async_remote_copy(
                src_ref=activ.at[:, pl.ds(pl.multiple_of(peer * width, width), width)],
                dst_ref=acts.at[me],
                send_sem=act_send.at[mask],
                recv_sem=act_recv.at[mask],
                device_id={"shard": peer},
                device_id_type=MESH,
            )
        )
        act_copies[-1].start()
    id_copies = []
    for d in range(1, reps):
        id_copies.append(
            pltpu.make_async_remote_copy(
                src_ref=chosen.at[0],
                dst_ref=got_ids.at[rep],
                send_sem=id_send.at[d],
                recv_sem=id_recv.at[d],
                device_id={"rep": lax.rem(rep + d, reps)},
                device_id_type=MESH,
            )
        )
        id_copies[-1].start()

    ids_row = chosen[0]
    got_ids[rep] = ids_row
    spread = jnp.broadcast_to(ids_row.astype(jnp.float32), (size, keep))
    columns_of[...] = spread.T.astype(jnp.int32)
    picked[...] = jnp.zeros_like(picked)
    loads[0].wait()
    step = 2 * size

    def pick(i, carry):
        base = pl.multiple_of(i * step, step)
        rows = table[pl.ds(base, step), :]
        lane = lax.broadcasted_iota(jnp.int32, (keep, size), 1) + base
        ids = columns_of[...]
        one_hot = jnp.concatenate(
            [
                jnp.where(ids == lane, 1.0, 0.0).astype(jnp.bfloat16),
                jnp.where(ids == lane + size, 1.0, 0.0).astype(jnp.bfloat16),
            ],
            axis=1,
        )
        picked[...] += jnp.dot(one_hot, rows, preferred_element_type=jnp.float32)
        line = lax.broadcasted_iota(jnp.int32, (step, keep), 0) + base
        taken = jnp.max(
            jnp.where(chosen[0] == line, 1.0, 0.0), axis=1, keepdims=True
        )
        cleared = jnp.where(taken > 0.5, 0.0, rows.astype(jnp.float32))
        table[pl.ds(base, step), :] = cleared.astype(jnp.bfloat16)
        return carry

    lax.fori_loop(0, count // step, pick, 0)
    got_rows[rep] = picked[...].astype(jnp.bfloat16)

    loads[2].wait()
    first.wait_recv()
    have, grad_copies = [0, bits[0]], [first]
    for bit in bits[1:]:
        wave = [grad_copy(h, bit) for h in have]
        for copy in wave:
            copy.start()
        for copy in wave:
            copy.wait_recv()
        grad_copies += wave
        have += [h + bit for h in have]

    loads[1].wait()
    part = largest_divisor(width, 512, 128)

    def columns(block, slot):
        def body(i, carry):
            at = pl.multiple_of(i * part, part)
            cols_out[slot, :, pl.ds(at, part)] = lax.dot_general(
                grads[block],
                weight[pl.ds(at, part), :],
                (((1,), (1,)), ((), ())),
                preferred_element_type=jnp.float32,
            ).astype(jnp.bfloat16)
            return carry

        lax.fori_loop(0, width // part, body, 0)

    mine = input_grad.at[:, pl.ds(pl.multiple_of(me * width, width), width)]
    for mask in masks:
        columns(flip(me, mask), mask)
    row_copies = []
    for d in range(1, reps):
        row_copies.append(
            pltpu.make_async_remote_copy(
                src_ref=got_rows.at[rep],
                dst_ref=got_rows.at[rep],
                send_sem=row_send.at[d],
                recv_sem=row_recv.at[d],
                device_id={"rep": lax.rem(rep + d, reps)},
                device_id_type=MESH,
            )
        )
        row_copies[-1].start()
    columns(me, 0)
    out_copies = []
    for mask in masks:
        out_copies.append(
            pltpu.make_async_remote_copy(
                src_ref=cols_out.at[mask],
                dst_ref=mine,
                send_sem=out_send.at[mask],
                recv_sem=out_recv.at[mask],
                device_id={"shard": flip(me, mask)},
                device_id_type=MESH,
            )
        )
        out_copies[-1].start()
    own_out = pltpu.make_async_copy(cols_out.at[0], mine, local_sem.at[1])
    own_out.start()

    for copy in id_copies:
        copy.wait_recv()
    for copy in row_copies:
        copy.wait_recv()
    lens = lengths[...]
    order = lax.broadcasted_iota(jnp.int32, lens.shape, 1)
    start = jnp.sum(jnp.where(order < rep, lens, 0), axis=1, keepdims=True)
    length = jnp.sum(jnp.where(order == rep, lens, 0), axis=1, keepdims=True)
    region = owned.shape[1]
    tall = largest_divisor(region, 256, 8)

    def gather_region(i, carry):
        base = pl.multiple_of(i * tall, 8)
        line = lax.broadcasted_iota(jnp.int32, (tall, keep), 0) + base

        def add(r, total):
            offset = got_ids[r] - start
            offset = jnp.where((offset >= 0) & (offset < length), offset, -1)
            one_hot = jnp.where(offset == line, 1.0, 0.0).astype(jnp.bfloat16)
            return total + jnp.dot(one_hot, got_rows[r], preferred_element_type=jnp.float32)

        owned_buf[pl.ds(base, tall), :] = lax.fori_loop(
            0, reps, add, jnp.zeros((tall, size), jnp.float32)
        )
        return carry

    lax.fori_loop(0, region // tall, gather_region, 0)
    own_sum = pltpu.make_async_copy(owned_buf, owned.at[0], local_sem.at[0])
    own_sum.start()

    loads[3].wait()
    for copy in act_copies:
        copy.wait_recv()
    chunk = largest_divisor(width, 256, 128)
    per_row = feats // size

    def update(i, carry):
        at = pl.multiple_of(i * chunk, chunk)
        left = acts[:, :, pl.ds(at, chunk)].reshape(n * tokens, chunk)
        right = grads[...].reshape(n * tokens, feats)
        grad = lax.dot_general(
            left, right, (((0,), (0,)), ((), ())), preferred_element_type=jnp.float32
        )
        for j in range(per_row):
            grad_blocks[pl.ds(j, chunk, stride=per_row), :] = grad[:, j * size : (j + 1) * size]
        rows = pl.ds(pl.multiple_of(i * chunk * per_row, chunk * per_row), chunk * per_row)
        table[rows, :] = (table[rows, :].astype(jnp.float32) + grad_blocks[...]).astype(
            jnp.bfloat16
        )
        return carry

    lax.fori_loop(0, width // chunk, update, 0)
    new_table = pltpu.make_async_copy(table, next_feedback.at[0], local_sem.at[2])
    new_table.start()

    own_out.wait()
    own_sum.wait()
    for copy in out_copies:
        copy.wait_recv()
    new_table.wait()
    for copy in grad_copies + act_copies + id_copies + row_copies + out_copies:
        copy.wait_send()


def solution(mesh):
    n, reps = mesh.shape["shard"], mesh.shape["rep"]

    def per_device(activ, key_grad, key_weight, feedback, kept, region_len):
        tokens, feats = key_grad.shape
        width = activ.shape[1] // n
        _, count, size = feedback.shape
        keep = kept.shape[-1]
        mean_len = count // reps
        region = mean_len + mean_len // 2
        dma = pltpu.SemaphoreType.DMA
        any_space = pl.BlockSpec(memory_space=pl.ANY)
        vmem = pl.BlockSpec(memory_space=pltpu.VMEM)
        bf16 = jnp.bfloat16
        return pl.pallas_call(
            functools.partial(kernel, n, reps),
            out_shape=(
                jax.ShapeDtypeStruct(activ.shape, bf16),
                jax.ShapeDtypeStruct(feedback.shape, bf16),
                jax.ShapeDtypeStruct((1, region, size), jnp.float32),
            ),
            in_specs=[any_space] * 4 + [vmem] * 2,
            out_specs=(any_space,) * 3,
            scratch_shapes=[
                pltpu.VMEM((n, tokens, feats), bf16),
                pltpu.VMEM((n, tokens, width), bf16),
                pltpu.VMEM((width, feats), bf16),
                pltpu.VMEM((count, size), bf16),
                pltpu.VMEM((reps, keep, size), bf16),
                pltpu.VMEM((reps, 1, keep), jnp.int32),
                pltpu.VMEM((n, tokens, width), bf16),
                pltpu.VMEM((keep, size), jnp.int32),
                pltpu.VMEM((keep, size), jnp.float32),
                pltpu.VMEM((largest_divisor(width, 256, 128) * (feats // size), size), jnp.float32),
                pltpu.VMEM((region, size), jnp.float32),
                dma((4,)),
                dma((n,)),
                dma((n,)),
                dma((n,)),
                dma((n,)),
                dma((n,)),
                dma((n,)),
                dma((reps,)),
                dma((reps,)),
                dma((reps,)),
                dma((reps,)),
            ],
            compiler_params=pltpu.CompilerParams(
                collective_id=0, has_side_effects=True, vmem_limit_bytes=48 * 1024 * 1024
            ),
        )(activ, key_grad, key_weight, feedback, kept, region_len)

    return jax.shard_map(
        per_device,
        mesh=mesh,
        in_specs=(
            P(("rep", "shard"), None),
            P(("rep", "shard"), None),
            P("shard", None),
            P("rep", "shard", None),
            P("rep", "shard", None),
            P("shard", None),
        ),
        out_specs=(P(("rep", "shard"), None), P("rep", "shard", None), P("shard", "rep", None)),
        check_vma=False,
    )
```

time: 119 us -> 73.6 us (0.62)
  the two profiles are of different devices: /device:TPU:0 before, /device:TPU:15 now
where the time goes in v1:
time: 73.6 us; the launch traced here: 73.4 us
  Pallas kernels  64 us (87%)
  local copies, waits for them, and re-layouts  8.76 us (12%)
    pallas_call x1, Pallas kernels, per_device(): pl.pallas_call(functools.partial(kernel, n, reps), out_shape=(jax.ShapeDt...  64 us
    unnamed x13, local copies, waits for them, and re-layouts  8.76 us

profile of v1, /device:TPU:15, one launch (start us, length us, event | category | flops | bytes accessed | tf_op | source)
XLA Modules:
  0.0 73.4 jit_solution(1180678803488008167)
XLA Ops:
  0.6 0.0 copy-start
  0.6 1.6 %copy-done = bf16[128,8192]{1,0:T(8,128)(2,1)S(1)} copy-done((bf16[128,8192]{1,0:T(8,128)(2,1)S(1)}, bf16[128,8192]{1,0:T(8,128)(2,1)}, u32[]{:S(2)}) %copy-start) | copy-done | bytes 2097176
  2.2 0.0 copy-start.1
  2.2 0.9 %copy-done.1 = bf16[128,640]{1,0:T(8,128)(2,1)S(1)} copy-done((bf16[128,640]{1,0:T(8,128)(2,1)S(1)}, bf16[128,640]{1,0:T(8,128)(2,1)}, u32[]{:S(2)}) %copy-start.1) | copy-done | bytes 163864
  3.1 0.0 copy-start.2
  3.1 0.7 copy-done.2
  3.8 0.0 copy-start.3
  3.8 0.7 copy-done.3
  4.5 64.0 %shard_map.85 = (bf16[128,8192]{1,0:T(8,128)(2,1)S(1)}, bf16[1,10240,128]{2,1,0:T(8,128)(2,1)}, f32[1,1920,128]{2,1,0:T(8,128)S(1)}) custom-call(bf16[128,8192]{1,0:T(8,128)(2,1)S(1)} %copy-done, bf16[128,640]{1,0:T(8,128)(2,1)S(1)} %copy-done.1, bf16[2048,640]{1,0:T(8,128)(2,1)} %key_weight.1, bf16[1,10240,128]{2,1,0:T(8,128)(2,1)} %feedback.1, ...), custom_call_target="tpu_custom_call" | custom-call | tf_op jit(solution)/shard_map/pallas_call | solution.py:315
  68.5 0.0 copy-start.4
  68.5 1.3 %copy.12 = bf16[128,8192]{1,0:T(8,128)(2,1)} copy(bf16[128,8192]{1,0:T(8,128)(2,1)S(1)} %get-tuple-element.6) | data formatting | bytes 4194304
  69.8 1.2 %copy-done.4 = bf16[1,10240,128]{2,1,0:T(8,128)(2,1)S(1)} copy-done((bf16[1,10240,128]{2,1,0:T(8,128)(2,1)S(1)}, bf16[1,10240,128]{2,1,0:T(8,128)(2,1)}, u32[]{:S(2)}) %copy-start.4) | copy-done | bytes 2621464
  71.0 1.5 %copy.13 = bf16[1,10240,128]{2,1,0:T(8,128)(2,1)} copy(bf16[1,10240,128]{2,1,0:T(8,128)(2,1)S(1)} %copy-done.4) | data formatting | bytes 5242880
  72.5 0.9 %copy.14 = f32[1,1920,128]{2,1,0:T(8,128)} copy(f32[1,1920,128]{2,1,0:T(8,128)S(1)} %get-tuple-element.8) | data formatting | bytes 1966080
Async XLA Ops:
  0.6 1.6 %copy-start = (bf16[128,8192]{1,0:T(8,128)(2,1)S(1)}, bf16[128,8192]{1,0:T(8,128)(2,1)}, u32[]{:S(2)}) copy-start(bf16[128,8192]{1,0:T(8,128)(2,1)} %activ.1) | copy-start | bytes 6291460
  2.2 0.9 %copy-start.1 = (bf16[128,640]{1,0:T(8,128)(2,1)S(1)}, bf16[128,640]{1,0:T(8,128)(2,1)}, u32[]{:S(2)}) copy-start(bf16[128,640]{1,0:T(8,128)(2,1)} %key_grad.1) | copy-start | bytes 491524
  3.1 0.7 copy-start.2
  3.8 0.7 copy-start.3
  68.5 2.5 %copy-start.4 = (bf16[1,10240,128]{2,1,0:T(8,128)(2,1)S(1)}, bf16[1,10240,128]{2,1,0:T(8,128)(2,1)}, u32[]{:S(2)}) copy-start(bf16[1,10240,128]{2,1,0:T(8,128)(2,1)} %get-tuple-element.7) | copy-start | bytes 7864324

commit v2 on v1

--- a/solution.py
+++ b/solution.py
@@ -35,8 +35,8 @@
     key_grad,
     key_weight,
     feedback,
-    chosen,
-    lengths,
+    kept,
+    region_len,
     input_grad,
     next_feedback,
     owned,
@@ -49,6 +49,8 @@
     cols_out,
     columns_of,
     picked,
+    chosen,
+    lengths,
     grad_blocks,
     owned_buf,
     local_sem,
@@ -68,7 +70,7 @@
     tokens, feats = key_grad.shape
     width = activ.shape[1] // n
     count, size = table.shape
-    keep = chosen.shape[-1]
+    keep = kept.shape[-1]
     masks = list(range(n - 1, 0, -1))
 
     loads = [
@@ -80,6 +82,8 @@
             acts.at[me],
             local_sem.at[3],
         ),
+        pltpu.make_async_copy(kept.at[0], chosen, local_sem.at[5]),
+        pltpu.make_async_copy(region_len, lengths, local_sem.at[6]),
     ]
     for load in loads:
         load.start()
@@ -131,8 +135,8 @@
     for d in range(1, reps):
         id_copies.append(
             pltpu.make_async_remote_copy(
-                src_ref=chosen.at[0],
-                dst_ref=got_ids.at[rep],
+                src_ref=kept.at[0, 0],
+                dst_ref=got_ids.at[rep, 0],
                 send_sem=id_send.at[d],
                 recv_sem=id_recv.at[d],
                 device_id={"rep": lax.rem(rep + d, reps)},
@@ -141,7 +145,9 @@
         )
         id_copies[-1].start()
 
-    ids_row = chosen[0]
+    loads[4].wait()
+    loads[5].wait()
+    ids_row = chosen[...]
     got_ids[rep] = ids_row
     spread = jnp.broadcast_to(ids_row.astype(jnp.float32), (size, keep))
     columns_of[...] = spread.T.astype(jnp.int32)
@@ -164,7 +170,7 @@
         picked[...] += jnp.dot(one_hot, rows, preferred_element_type=jnp.float32)
         line = lax.broadcasted_iota(jnp.int32, (step, keep), 0) + base
         taken = jnp.max(
-            jnp.where(chosen[0] == line, 1.0, 0.0), axis=1, keepdims=True
+            jnp.where(chosen[...] == line, 1.0, 0.0), axis=1, keepdims=True
         )
         cleared = jnp.where(taken > 0.5, 0.0, rows.astype(jnp.float32))
         table[pl.ds(base, step), :] = cleared.astype(jnp.bfloat16)
@@ -185,25 +191,6 @@
         grad_copies += wave
         have += [h + bit for h in have]
 
-    loads[1].wait()
-    part = largest_divisor(width, 512, 128)
-
-    def columns(block, slot):
-        def body(i, carry):
-            at = pl.multiple_of(i * part, part)
-            cols_out[slot, :, pl.ds(at, part)] = lax.dot_general(
-                grads[block],
-                weight[pl.ds(at, part), :],
-                (((1,), (1,)), ((), ())),
-                preferred_element_type=jnp.float32,
-            ).astype(jnp.bfloat16)
-            return carry
-
-        lax.fori_loop(0, width // part, body, 0)
-
-    mine = input_grad.at[:, pl.ds(pl.multiple_of(me * width, width), width)]
-    for mask in masks:
-        columns(flip(me, mask), mask)
     row_copies = []
     for d in range(1, reps):
         row_copies.append(
@@ -217,6 +204,26 @@
             )
         )
         row_copies[-1].start()
+
+    loads[1].wait()
+    part = largest_divisor(width, 512, 128)
+
+    def columns(block, slot):
+        def body(i, carry):
+            at = pl.multiple_of(i * part, part)
+            cols_out[slot, :, pl.ds(at, part)] = lax.dot_general(
+                grads[block],
+                weight[pl.ds(at, part), :],
+                (((1,), (1,)), ((), ())),
+                preferred_element_type=jnp.float32,
+            ).astype(jnp.bfloat16)
+            return carry
+
+        lax.fori_loop(0, width // part, body, 0)
+
+    mine = input_grad.at[:, pl.ds(pl.multiple_of(me * width, width), width)]
+    for mask in masks:
+        columns(flip(me, mask), mask)
     columns(me, 0)
     out_copies = []
     for mask in masks:
@@ -234,6 +241,31 @@
     own_out = pltpu.make_async_copy(cols_out.at[0], mine, local_sem.at[1])
     own_out.start()
 
+    loads[3].wait()
+    for copy in act_copies:
+        copy.wait_recv()
+    chunk = largest_divisor(width, 256, 128)
+    per_row = feats // size
+
+    def update(i, carry):
+        at = pl.multiple_of(i * chunk, chunk)
+        left = acts[:, :, pl.ds(at, chunk)].reshape(n * tokens, chunk)
+        right = grads[...].reshape(n * tokens, feats)
+        grad = lax.dot_general(
+            left, right, (((0,), (0,)), ((), ())), preferred_element_type=jnp.float32
+        )
+        for j in range(per_row):
+            grad_blocks[pl.ds(j, chunk, stride=per_row), :] = grad[:, j * size : (j + 1) * size]
+        rows = pl.ds(pl.multiple_of(i * chunk * per_row, chunk * per_row), chunk * per_row)
+        table[rows, :] = (table[rows, :].astype(jnp.float32) + grad_blocks[...]).astype(
+            jnp.bfloat16
+        )
+        return carry
+
+    lax.fori_loop(0, width // chunk, update, 0)
+    new_table = pltpu.make_async_copy(table, next_feedback.at[0], local_sem.at[2])
+    new_table.start()
+
     for copy in id_copies:
         copy.wait_recv()
     for copy in row_copies:
@@ -264,31 +296,6 @@
     own_sum = pltpu.make_async_copy(owned_buf, owned.at[0], local_sem.at[0])
     own_sum.start()
 
-    loads[3].wait()
-    for copy in act_copies:
-        copy.wait_recv()
-    chunk = largest_divisor(width, 256, 128)
-    per_row = feats // size
-
-    def update(i, carry):
-        at = pl.multiple_of(i * chunk, chunk)
-        left = acts[:, :, pl.ds(at, chunk)].reshape(n * tokens, chunk)
-        right = grads[...].reshape(n * tokens, feats)
-        grad = lax.dot_general(
-            left, right, (((0,), (0,)), ((), ())), preferred_element_type=jnp.float32
-        )
-        for j in range(per_row):
-            grad_blocks[pl.ds(j, chunk, stride=per_row), :] = grad[:, j * size : (j + 1) * size]
-        rows = pl.ds(pl.multiple_of(i * chunk * per_row, chunk * per_row), chunk * per_row)
-        table[rows, :] = (table[rows, :].astype(jnp.float32) + grad_blocks[...]).astype(
-            jnp.bfloat16
-        )
-        return carry
-
-    lax.fori_loop(0, width // chunk, update, 0)
-    new_table = pltpu.make_async_copy(table, next_feedback.at[0], local_sem.at[2])
-    new_table.start()
-
     own_out.wait()
     own_sum.wait()
     for copy in out_copies:
@@ -310,7 +317,6 @@
         region = mean_len + mean_len // 2
         dma = pltpu.SemaphoreType.DMA
         any_space = pl.BlockSpec(memory_space=pl.ANY)
-        vmem = pl.BlockSpec(memory_space=pltpu.VMEM)
         bf16 = jnp.bfloat16
         return pl.pallas_call(
             functools.partial(kernel, n, reps),
@@ -319,7 +325,7 @@
                 jax.ShapeDtypeStruct(feedback.shape, bf16),
                 jax.ShapeDtypeStruct((1, region, size), jnp.float32),
             ),
-            in_specs=[any_space] * 4 + [vmem] * 2,
+            in_specs=[any_space] * 6,
             out_specs=(any_space,) * 3,
             scratch_shapes=[
                 pltpu.VMEM((n, tokens, feats), bf16),
@@ -331,9 +337,11 @@
                 pltpu.VMEM((n, tokens, width), bf16),
                 pltpu.VMEM((keep, size), jnp.int32),
                 pltpu.VMEM((keep, size), jnp.float32),
+                pltpu.VMEM((1, keep), jnp.int32),
+                pltpu.VMEM((1, reps), jnp.int32),
                 pltpu.VMEM((largest_divisor(width, 256, 128) * (feats // size), size), jnp.float32),
                 pltpu.VMEM((region, size), jnp.float32),
-                dma((4,)),
+                dma((7,)),
                 dma((n,)),
                 dma((n,)),
                 dma((n,)),
@@ -346,7 +354,7 @@
                 dma((reps,)),
             ],
             compiler_params=pltpu.CompilerParams(
-                collective_id=0, has_side_effects=True, vmem_limit_bytes=48 * 1024 * 1024
+                collective_id=0, has_side_effects=True, vmem_limit_bytes=67043328
             ),
         )(activ, key_grad, key_weight, feedback, kept, region_len)
 

time: 73.6 us -> 64.3 us (0.87)
  the two profiles are of different devices: /device:TPU:15 before, /device:TPU:0 now
where the time goes in v2:
time: 64.3 us; the launch traced here: 64.1 us
  Pallas kernels  57.4 us (89%)
  local copies, waits for them, and re-layouts  6.08 us (9%)
  between operations  0.65 us (1%)
    pallas_call x1, Pallas kernels, per_device(): pl.pallas_call(functools.partial(kernel, n, reps), out_shape=(jax.ShapeDt...  57.4 us
    unnamed x7, local copies, waits for them, and re-layouts  6.08 us

profile of v2, /device:TPU:0, one launch (start us, length us, event | category | flops | bytes accessed | tf_op | source)
XLA Modules:
  0.0 64.1 jit_solution(17406101006096956543)
XLA Ops:
  0.6 57.4 %shard_map.85 = (bf16[128,8192]{1,0:T(8,128)(2,1)}, bf16[1,10240,128]{2,1,0:T(8,128)(2,1)}, f32[1,1920,128]{2,1,0:T(8,128)}) custom-call(bf16[128,8192]{1,0:T(8,128)(2,1)} %activ.1, bf16[128,640]{1,0:T(8,128)(2,1)} %key_grad.1, bf16[2048,640]{1,0:T(8,128)(2,1)} %key_weight.1, bf16[1,10240,128]{2,1,0:T(8,128)(2,1)} %feedback.1, s32[1,1,512]{2,1,0:T(1,128)} %kept.1, ...), custom_call_target="tpu_custom_call" | custom-call | tf_op jit(solution)/shard_map/pallas_call | solution.py:321
  58.0 0.0 copy-start
  58.0 3.2 %copy.12 = bf16[128,8192]{1,0:T(8,128)(2,1)} copy(bf16[128,8192]{1,0:T(8,128)(2,1)} %get-tuple-element.6) | data formatting | bytes 4194304
  61.2 0.0 copy-done
  61.2 0.0 copy-start.1
  61.3 1.5 %copy.13 = bf16[1,10240,128]{2,1,0:T(8,128)(2,1)} copy(bf16[1,10240,128]{2,1,0:T(8,128)(2,1)S(1)} %copy-done) | data formatting | bytes 5242880
  62.7 0.4 copy-done.1
  63.1 0.9 %copy.14 = f32[1,1920,128]{2,1,0:T(8,128)} copy(f32[1,1920,128]{2,1,0:T(8,128)S(1)} %copy-done.1) | data formatting | bytes 1966080
Async XLA Ops:
  58.0 3.3 %copy-start = (bf16[1,10240,128]{2,1,0:T(8,128)(2,1)S(1)}, bf16[1,10240,128]{2,1,0:T(8,128)(2,1)}, u32[]{:S(2)}) copy-start(bf16[1,10240,128]{2,1,0:T(8,128)(2,1)} %get-tuple-element.7) | copy-start | bytes 7864324
  61.2 1.9 %copy-start.1 = (f32[1,1920,128]{2,1,0:T(8,128)S(1)}, f32[1,1920,128]{2,1,0:T(8,128)}, u32[]{:S(2)}) copy-start(f32[1,1920,128]{2,1,0:T(8,128)} %get-tuple-element.8) | copy-start | bytes 2949124
